TPU v7x, 32 devices: a whole 2x2x4 slice. The times are simulated.
32 devices in a mesh: row: 8 (over z, x), col: 4 (over y, core).
Axes of the slice: x: 2, y: 2, z: 4, core: 2. Of those that a mesh axis runs over, the one named last changes fastest.
Arguments:
- tensor: float32 [32, 1024, 1024], P(None, 'row', 'col'), may hold values from -6 to 6
- initial_first: float32 [1024, 256], P('row'), may hold values from -6 to 6
- initial_second: float32 [1024, 256], P('col'), may hold values from -6 to 6
Outputs:
- factor_first: float32 [1024, 256], P('row')
- factor_second: float32 [1024, 256], P('col')
- factor_frames: float32 [32, 256], replicated
- weights: float32 [256], replicated
All inputs are finite; a program needn't handle non-finite values.
Results may differ from a plain program's by a relative error of at most 0.00024.
Values sent between devices are 32-bit elements; how exact they have to be, the bound alone decides.
A program may use at most 128 MiB of HBM per device.

v0:
```python
import math
import jax
import jax.numpy as jnp
from jax import lax
from jax.sharding import PartitionSpec as P

PASSES = 2
epsilon = 1e-06


def solve_gram(partials, hadamard):
    factor_lower = jnp.linalg.cholesky(hadamard)
    midway = lax.linalg.triangular_solve(
        factor_lower, partials, left_side=False, lower=True, transpose_a=True
    )
    return lax.linalg.triangular_solve(
        factor_lower, midway, left_side=False, lower=True, transpose_a=False
    )


def local_gram(matrix):
    return jnp.dot(matrix.T, matrix, precision=lax.Precision.HIGHEST)


def normalize_second(unscaled, row_count):
    squares = lax.psum(jnp.sum(unscaled * unscaled, axis=0), "col")
    scaling = jnp.sqrt(squares / row_count + epsilon)
    normed = unscaled / scaling
    gram_new = lax.psum(local_gram(normed), "col") / row_count
    return (normed, gram_new)


def body(tensor, initial_first, initial_second):
    highest = lax.Precision.HIGHEST
    frames = tensor.shape[0]
    rows_first = tensor.shape[1] * lax.axis_size("row")
    rows_second = tensor.shape[2] * lax.axis_size("col")
    first_gram = lax.psum(local_gram(initial_first), "row") / rows_first
    second = initial_second
    second_gram = lax.psum(local_gram(initial_second), "col") / rows_second
    contracted = jnp.einsum("kij,ir->kjr", tensor, initial_first, precision=highest)
    for repeat in range(PASSES):
        frame_terms = jnp.einsum("kjr,jr->kr", contracted, second, precision=highest)
        frame_sums = lax.psum(frame_terms, ("row", "col"))
        frame_raw = solve_gram(frame_sums, first_gram * second_gram) / math.sqrt(
            rows_first * rows_second
        )
        frame_scaling = jnp.sqrt(jnp.mean(frame_raw * frame_raw, axis=0) + epsilon)
        factor_frames = frame_raw / frame_scaling
        frame_gram = local_gram(factor_frames) / frames
        second_terms = jnp.einsum("kjr,kr->jr", contracted, factor_frames, precision=highest)
        hadamard = first_gram * frame_gram
        own_rows = lax.psum_scatter(second_terms, "row", scatter_dimension=0, tiled=True)
        solved_rows = solve_gram(own_rows, hadamard) / math.sqrt(rows_first * frames)
        second_raw = lax.all_gather(solved_rows, "row", axis=0, tiled=True)
        second, second_gram = normalize_second(second_raw, rows_second)
    second_contracted = jnp.einsum("kij,jr->kir", tensor, second, precision=highest)
    first_terms = jnp.einsum("kir,kr->ir", second_contracted, factor_frames, precision=highest)
    hadamard = second_gram * frame_gram
    own_rows = lax.psum_scatter(first_terms, "col", scatter_dimension=0, tiled=True)
    solved_rows = solve_gram(own_rows, hadamard) / math.sqrt(rows_second * frames)
    first_raw = lax.all_gather(solved_rows, "col", axis=0, tiled=True)
    squares = lax.psum(jnp.sum(first_raw * first_raw, axis=0), "row")
    weights = jnp.sqrt(squares / rows_first + epsilon)
    factor_first = first_raw / weights
    return (factor_first, second, factor_frames, weights)


def solution(mesh):
    placed = (P(None, "row", "col"), P("row", None), P("col", None))
    return jax.shard_map(
        body,
        mesh=mesh,
        in_specs=placed,
        out_specs=(P("row", None), P("col", None), P(), P()),
        check_vma=False,
    )
```

profile of v0, /device:TPU:0, one launch (start us, length us, event | category | flops | bytes accessed | tf_op | source)
XLA Modules:
  0.0 647.6 jit_solution(8311122888523446965)
XLA Ops:
  10.9 10.7 %multiply_reduce_fusion.3 = (f32[256,32]{0,1:T(8,128)S(1)}, f32[32,256,256]{2,1,0:T(8,128)}) fusion(f32[256,256]{0,1:T(8,128)} %bitcast.270, f32[32,128,256]{2,1,0:T(8,128)} %param.8, f32[128,256]{1,0:T(8,128)S(1)} %copy-done), kind=kOutput, calls=%fused_computation.13 | convolution fusion | flops 3225411584 | bytes 13008896 | tf_op jit(solution)/shard_map/kij,ir->kjr/dot_general | solution.py:41
  21.7 43.2 %psum.65 = f32[32,256]{0,1:T(8,128)S(1)} all-reduce(f32[32,256]{0,1:T(8,128)S(1)} %bitcast.276), channel_id=1, replica_groups=mesh['row'=8,'col'=4] {'row','col'}, use_global_device_ids=true, to_apply=%region_6.0 | all-reduce | flops 8192 | bytes 65536 | tf_op jit(solution)/shard_map/psum | solution.py:44
  65.0 55.4 %all-reduce.6.cloned.1.call-done = f32[256,256]{0,1:T(8,128)} async-done(((f32[256,256]{0,1:T(8,128)}), f32[256,256]{0,1:T(8,128)}) %all-reduce.6.cloned.1.call-update) | async-done | bytes 262160 | tf_op jit(solution)/shard_map/psum | solution.py:38
  121.7 11.7 %cholesky.256 = f32[128,128]{1,0:T(8,128)S(1)} custom-call(f32[128,128]{1,0:T(8,128)S(1)} %cholesky.422), custom_call_target="Cholesky" | custom-call | tf_op jit(solution)/shard_map/jit(cholesky)/cholesky | solution.py:12
  133.5 9.8 %custom-call.26 = f32[1,128,128]{1,2,0:T(8,128)S(1)} custom-call(f32[1,128,128]{2,1,0:T(8,128)S(1)} %get-tuple-element.150), custom_call_target="InvertDiagBlocksLowerTriangular" | custom-call | tf_op jit(solution)/shard_map/jit(cholesky)/cholesky | solution.py:12
  143.8 11.7 %cholesky.273 = f32[128,128]{1,0:T(8,128)S(1)} custom-call(f32[128,128]{1,0:T(8,128)S(1)} %convolution_subtract_fusion.9), custom_call_target="Cholesky" | custom-call | tf_op jit(solution)/shard_map/jit(cholesky)/cholesky | solution.py:12
  161.6 20.1 %custom-call.27 = f32[2,128,128]{1,2,0:T(8,128)S(1)} custom-call(f32[2,128,128]{2,1,0:T(8,128)S(1)} %get-tuple-element.71), custom_call_target="InvertDiagBlocksLowerTriangular" | custom-call | tf_op jit(solution)/shard_map/triangular_solve/custom-call.0 | solution.py:13
  188.7 11.7 %cholesky.290 = f32[128,128]{1,0:T(8,128)S(1)} custom-call(f32[128,128]{1,0:T(8,128)S(1)} %cholesky.425), custom_call_target="Cholesky" | custom-call | tf_op jit(solution)/shard_map/jit(cholesky)/cholesky | solution.py:12
  200.5 9.8 %custom-call.29 = f32[1,128,128]{1,2,0:T(8,128)S(1)} custom-call(f32[1,128,128]{2,1,0:T(8,128)S(1)} %get-tuple-element.146), custom_call_target="InvertDiagBlocksLowerTriangular" | custom-call | tf_op jit(solution)/shard_map/jit(cholesky)/cholesky | solution.py:12
  210.8 11.7 %cholesky.307 = f32[128,128]{1,0:T(8,128)S(1)} custom-call(f32[128,128]{1,0:T(8,128)S(1)} %convolution_subtract_fusion.7), custom_call_target="Cholesky" | custom-call | tf_op jit(solution)/shard_map/jit(cholesky)/cholesky | solution.py:12
  229.3 19.7 %custom-call.30 = f32[2,128,128]{1,2,0:T(8,128)S(1)} custom-call(f32[2,128,128]{2,1,0:T(8,128)S(1)} %get-tuple-element.73), custom_call_target="InvertDiagBlocksLowerTriangular" | custom-call | tf_op jit(solution)/shard_map/triangular_solve/custom-call.0 | solution.py:13
  252.6 30.9 %all_gather.9 = f32[256,256]{1,0:T(8,128)S(1)} all-gather(f32[32,256]{1,0:T(8,128)S(1)} %maximum_multiply_fusion.1), channel_id=1, replica_groups=mesh['row'=8,'col'=4] {'row'}, dimensions={0}, use_global_device_ids=true | all-gather | bytes 294912 | tf_op jit(solution)/shard_map/all_gather | solution.py:55
  283.5 5.7 psum.66
  294.9 39.1 %psum.68 = f32[32,256]{0,1:T(8,128)S(1)} all-reduce(f32[32,256]{0,1:T(8,128)S(1)} %bitcast.277), channel_id=1, replica_groups=mesh['row'=8,'col'=4] {'row','col'}, use_global_device_ids=true, to_apply=%region_12.16 | all-reduce | flops 8192 | bytes 65536 | tf_op jit(solution)/shard_map/psum | solution.py:44
  335.3 11.7 %cholesky.324 = f32[128,128]{1,0:T(8,128)S(1)} custom-call(f32[128,128]{1,0:T(8,128)S(1)} %cholesky.428), custom_call_target="Cholesky" | custom-call | tf_op jit(solution)/shard_map/jit(cholesky)/cholesky | solution.py:12
  347.0 9.8 %custom-call.32 = f32[1,128,128]{1,2,0:T(8,128)S(1)} custom-call(f32[1,128,128]{2,1,0:T(8,128)S(1)} %get-tuple-element.142), custom_call_target="InvertDiagBlocksLowerTriangular" | custom-call | tf_op jit(solution)/shard_map/jit(cholesky)/cholesky | solution.py:12
  357.3 11.7 %cholesky.341 = f32[128,128]{1,0:T(8,128)S(1)} custom-call(f32[128,128]{1,0:T(8,128)S(1)} %convolution_subtract_fusion.5), custom_call_target="Cholesky" | custom-call | tf_op jit(solution)/shard_map/jit(cholesky)/cholesky | solution.py:12
  375.7 20.1 %custom-call.33 = f32[2,128,128]{1,2,0:T(8,128)S(1)} custom-call(f32[2,128,128]{2,1,0:T(8,128)S(1)} %get-tuple-element.75), custom_call_target="InvertDiagBlocksLowerTriangular" | custom-call | tf_op jit(solution)/shard_map/triangular_solve/custom-call.0 | solution.py:13
  402.9 11.7 %cholesky.358 = f32[128,128]{1,0:T(8,128)S(1)} custom-call(f32[128,128]{1,0:T(8,128)S(1)} %cholesky.431), custom_call_target="Cholesky" | custom-call | tf_op jit(solution)/shard_map/jit(cholesky)/cholesky | solution.py:12
  414.7 9.8 %custom-call.35 = f32[1,128,128]{1,2,0:T(8,128)S(1)} custom-call(f32[1,128,128]{2,1,0:T(8,128)S(1)} %get-tuple-element.138), custom_call_target="InvertDiagBlocksLowerTriangular" | custom-call | tf_op jit(solution)/shard_map/jit(cholesky)/cholesky | solution.py:12
  424.9 11.7 %cholesky.375 = f32[128,128]{1,0:T(8,128)S(1)} custom-call(f32[128,128]{1,0:T(8,128)S(1)} %convolution_subtract_fusion.3), custom_call_target="Cholesky" | custom-call | tf_op jit(solution)/shard_map/jit(cholesky)/cholesky | solution.py:12
  443.5 19.7 %custom-call.36 = f32[2,128,128]{1,2,0:T(8,128)S(1)} custom-call(f32[2,128,128]{2,1,0:T(8,128)S(1)} %get-tuple-element.77), custom_call_target="InvertDiagBlocksLowerTriangular" | custom-call | tf_op jit(solution)/shard_map/triangular_solve/custom-call.0 | solution.py:13
  468.9 30.9 %all_gather.10 = f32[256,256]{1,0:T(8,128)S(1)} all-gather(f32[32,256]{1,0:T(8,128)S(1)} %maximum_multiply_fusion.3), channel_id=1, replica_groups=mesh['row'=8,'col'=4] {'row'}, dimensions={0}, use_global_device_ids=true | all-gather | bytes 294912 | tf_op jit(solution)/shard_map/all_gather | solution.py:55
  499.8 5.7 psum.69
  505.5 10.0 %fusion.4 = f32[256,32,128]{2,0,1:T(8,128)} fusion(f32[32,128,256]{2,1,0:T(8,128)} %param.8, f32[256,256]{1,0:T(8,128)S(1)} %broadcast_divide_fusion), kind=kOutput, calls=%fused_computation.40 | convolution fusion | flops 3221225472 | bytes 8650752 | tf_op jit(solution)/shard_map/kij,jr->kir/dot_general | solution.py:57
  516.8 8.2 %fusion = f32[256,1,128]{2,1,0:T(1,128)S(1)} fusion(f32[32,256,1]{0,2,1:T(1,128)S(1)} %copy.67, f32[256,32,128]{2,0,1:T(8,128)} %fusion.4), kind=kOutput, calls=%fused_computation.14 | convolution fusion | flops 12582912 | bytes 4358144 | tf_op jit(solution)/shard_map/kir,kr->ir/dot_general | solution.py:58
  525.8 22.6 %all-reduce.12.cloned.1.call-done = f32[256,256]{0,1:T(8,128)} async-done(((f32[256,256]{0,1:T(8,128)}), f32[256,256]{0,1:T(8,128)}) %all-reduce.12.cloned.1.call-update) | async-done | bytes 262160 | tf_op jit(solution)/shard_map/psum | solution.py:29
  549.7 11.7 %cholesky.392 = f32[128,128]{1,0:T(8,128)S(1)} custom-call(f32[128,128]{1,0:T(8,128)S(1)} %cholesky.434), custom_call_target="Cholesky" | custom-call | tf_op jit(solution)/shard_map/jit(cholesky)/cholesky | solution.py:12
  561.4 9.8 %custom-call.38 = f32[1,128,128]{1,2,0:T(8,128)S(1)} custom-call(f32[1,128,128]{2,1,0:T(8,128)S(1)} %get-tuple-element.134), custom_call_target="InvertDiagBlocksLowerTriangular" | custom-call | tf_op jit(solution)/shard_map/jit(cholesky)/cholesky | solution.py:12
  571.7 11.7 %cholesky.409 = f32[128,128]{1,0:T(8,128)S(1)} custom-call(f32[128,128]{1,0:T(8,128)S(1)} %convolution_subtract_fusion.1), custom_call_target="Cholesky" | custom-call | tf_op jit(solution)/shard_map/jit(cholesky)/cholesky | solution.py:12
  590.2 19.9 %custom-call.39 = f32[2,128,128]{1,2,0:T(8,128)S(1)} custom-call(f32[2,128,128]{2,1,0:T(8,128)S(1)} %get-tuple-element.79), custom_call_target="InvertDiagBlocksLowerTriangular" | custom-call | tf_op jit(solution)/shard_map/triangular_solve/custom-call.0 | solution.py:13
  618.4 21.4 %psum.71 = f32[256]{0:T(256)S(1)} all-reduce(f32[256]{0:T(256)S(1)} %multiply_reduce_fusion.6), channel_id=1, replica_groups=mesh['row'=8,'col'=4] {'row'}, use_global_device_ids=true, to_apply=%region_20.24 | all-reduce | flops 256 | bytes 2048 | tf_op jit(solution)/shard_map/psum | solution.py:63
  (196 shorter events, 96.3 us)
Async XLA Ops:
  7.2 2.5 copy-start
  7.2 57.8 %all-reduce.8.cloned.1.call-start = ((), (), s32[]{:S(2)}) async-start(), calls=%async_computation.4 | async-start | bytes 524288 | tf_op jit(solution)/shard_map/psum | solution.py:40
  9.6 110.8 %all-reduce.6.cloned.1.call-start = ((), (), s32[]{:S(2)}) async-start(), calls=%async_computation.3 | async-start | bytes 524288 | tf_op jit(solution)/shard_map/psum | solution.py:38
  10.8 239.0 %reduce-scatter.10.cloned.1.call-start = ((), (), s32[]{:S(2)}) async-start(), calls=%async_computation.7 | async-start | bytes 294912
  120.4 67.6 %copy-start.1 = (f32[256,256]{0,1:T(8,128)S(1)}, f32[256,256]{0,1:T(8,128)}, u32[]{:S(2)}) copy-start(f32[256,256]{0,1:T(8,128)} %all-reduce.6.cloned.1.call-done) | copy-start | bytes 786436
  188.0 146.1 %all-reduce.10.cloned.1.call-start = ((), (), s32[]{:S(2)}) async-start(), calls=%async_computation.5 | async-start | bytes 524288 | tf_op jit(solution)/shard_map/psum | solution.py:29
  290.6 175.4 %reduce-scatter.12.cloned.1.call-start = ((), (), s32[]{:S(2)}) async-start(), calls=%async_computation.8 | async-start | bytes 294912
  397.2 118.2 %copy-start.3 = (f32[32,256]{1,0:T(8,128)}, f32[32,256]{1,0:T(8,128)S(1)}, u32[]{:S(2)}) copy-start(f32[32,256]{1,0:T(8,128)S(1)} %fusion.78) | copy-start | bytes 98308
  402.2 146.3 %all-reduce.12.cloned.1.call-start = ((), (), s32[]{:S(2)}) async-start(), calls=%async_computation.6 | async-start | bytes 524288 | tf_op jit(solution)/shard_map/psum | solution.py:29
  505.5 44.2 %copy-start.2 = (f32[256,256]{1,0:T(8,128)}, f32[256,256]{1,0:T(8,128)S(1)}, u32[]{:S(2)}) copy-start(f32[256,256]{1,0:T(8,128)S(1)} %broadcast_divide_fusion) | copy-start | bytes 786436
  516.8 93.4 %reduce-scatter.14.cloned.1.call-start = ((), (), s32[]{:S(2)}) async-start(), calls=%async_computation.9 | async-start | bytes 163840
  639.8 0.7 copy-start.4
Sparse Core Ops, SparseCore 0:
  10.9 34.9 all-reduce.7
  49.3 71.0 all-reduce.5
  188.1 61.6 reduce-scatter.9
  290.7 31.6 all-reduce.9
  402.3 63.6 reduce-scatter.11
  516.9 31.5 all-reduce.11
  551.5 19.8 reduce-scatter.13
where the time goes:
time: 653 us; the launch traced here: 648 us
  other arithmetic  290 us (44%)
  blocking collectives  182 us (28%)
  waiting for transfers between devices  81.9 us (13%)
  matrix products  46.5 us (7%)
  local copies, waits for them, and re-layouts  24.2 us (4%)
  between operations  21.7 us (3%)
    another operation x34, other arithmetic, solve_gram(): factor_lower = jnp.linalg.cholesky(hadamard)  172 us
    another operation x11, other arithmetic, solve_gram(): lax.linalg.triangular_solve(factor_lower, partials, left_side=False, lowe...  99.6 us
    psum x2, blocking collectives, body(): frame_sums = lax.psum(frame_terms, ('row', 'col'))  82.3 us
    all_gather x2, blocking collectives, body(): second_raw = lax.all_gather(solved_rows, 'row', axis=0, tiled=True)  61.7 us
    psum x1, waiting for transfers between devices, body(): first_gram = lax.psum(local_gram(initial_first), 'row') / rows_first  55.4 us
    psum x2, waiting for transfers between devices, normalize_second(): gram_new = lax.psum(local_gram(normed), 'col') / row_count  22.7 us
    another operation x39, local copies, waits for them, and re-layouts, solve_gram(): lax.linalg.triangular_solve(factor_lower, partials, left_side=False, lowe...  22 us
    psum x1, blocking collectives, body(): squares = lax.psum(jnp.sum(first_raw * first_raw, axis=0), 'row')  21.4 us
  transfers between devices with their start and end apart: 7, of which 4 were waited for; matrix products, arithmetic and copies ran while one was open for 32% of the time, Pallas kernels for 0%

commit v1 on v0

--- a/solution.py
+++ b/solution.py
@@ -35,7 +35,7 @@
     frames = tensor.shape[0]
     rows_first = tensor.shape[1] * lax.axis_size("row")
     rows_second = tensor.shape[2] * lax.axis_size("col")
-    first_gram = lax.psum(local_gram(initial_first), "row") / rows_first
+    first_gram = jnp.sum(lax.all_gather(local_gram(initial_first), "row"), axis=0) / rows_first
     second = initial_second
     second_gram = lax.psum(local_gram(initial_second), "col") / rows_second
     contracted = jnp.einsum("kij,ir->kjr", tensor, initial_first, precision=highest)

time: 653 us -> 674 us (1.032)
  waiting for transfers between devices: 81.9 us -> 98.1 us
    unnamed x10, waiting for transfers between devices: 3.8 us -> 75.7 us
    psum x1 -> x0, waiting for transfers between devices: 55.4 us -> none  [body(): first_gram = lax.psum(local_gram(initial_first), 'row') / rows_first]
  transfers between devices with their start and end apart: 7 -> 7, of which waited for: 4 -> 3; matrix products, arithmetic and copies ran while one was open for 32% -> 20% of each run, Pallas kernels for 0% -> 0%
where the time goes in v1:
time: 674 us; the launch traced here: 669 us
  other arithmetic  292 us (43%)
  blocking collectives  184 us (27%)
  waiting for transfers between devices  98.1 us (15%)
  matrix products  46.4 us (7%)
  local copies, waits for them, and re-layouts  25.1 us (4%)
  between operations  23 us (3%)
    another operation x34, other arithmetic, solve_gram(): factor_lower = jnp.linalg.cholesky(hadamard)  172 us
    another operation x11, other arithmetic, solve_gram(): lax.linalg.triangular_solve(factor_lower, partials, left_side=False, lowe...  99.6 us
    psum x2, blocking collectives, body(): frame_sums = lax.psum(frame_terms, ('row', 'col'))  83.7 us
    unnamed x10, waiting for transfers between devices  75.7 us
    all_gather x2, blocking collectives, body(): second_raw = lax.all_gather(solved_rows, 'row', axis=0, tiled=True)  61.8 us
    psum x2, waiting for transfers between devices, normalize_second(): gram_new = lax.psum(local_gram(normed), 'col') / row_count  22.3 us
    another operation x39, local copies, waits for them, and re-layouts, solve_gram(): lax.linalg.triangular_solve(factor_lower, partials, left_side=False, lowe...  22 us
    psum x1, blocking collectives, body(): squares = lax.psum(jnp.sum(first_raw * first_raw, axis=0), 'row')  21.4 us
  transfers between devices with their start and end apart: 7, of which 3 were waited for; matrix products, arithmetic and copies ran while one was open for 20% of the time, Pallas kernels for 0%

profile of v1, /device:TPU:0, one launch (start us, length us, event | category | flops | bytes accessed | tf_op | source)
XLA Modules:
  0.0 669.0 jit_solution(1148505227118449642)
XLA Ops:
  12.5 10.7 %multiply_reduce_fusion.3 = (f32[256,32]{0,1:T(8,128)S(1)}, f32[32,256,256]{2,1,0:T(8,128)}) fusion(f32[256,256]{0,1:T(8,128)} %bitcast.271, f32[32,128,256]{2,1,0:T(8,128)} %param.8, f32[128,256]{1,0:T(8,128)S(1)} %copy-done), kind=kOutput, calls=%fused_computation.13 | convolution fusion | flops 3225411584 | bytes 13008896 | tf_op jit(solution)/shard_map/kij,ir->kjr/dot_general | solution.py:41
  23.3 44.8 %psum.57 = f32[32,256]{0,1:T(8,128)S(1)} all-reduce(f32[32,256]{0,1:T(8,128)S(1)} %bitcast.278), channel_id=1, replica_groups=mesh['row'=8,'col'=4] {'row','col'}, use_global_device_ids=true, to_apply=%region_6.0 | all-reduce | flops 8192 | bytes 65536 | tf_op jit(solution)/shard_map/psum | solution.py:44
  71.3 11.7 %cholesky.256 = f32[128,128]{1,0:T(8,128)S(1)} custom-call(f32[128,128]{1,0:T(8,128)S(1)} %cholesky.422), custom_call_target="Cholesky" | custom-call | tf_op jit(solution)/shard_map/jit(cholesky)/cholesky | solution.py:12
  83.1 9.8 %custom-call.26 = f32[1,128,128]{1,2,0:T(8,128)S(1)} custom-call(f32[1,128,128]{2,1,0:T(8,128)S(1)} %get-tuple-element.150), custom_call_target="InvertDiagBlocksLowerTriangular" | custom-call | tf_op jit(solution)/shard_map/jit(cholesky)/cholesky | solution.py:12
  93.4 11.7 %cholesky.273 = f32[128,128]{1,0:T(8,128)S(1)} custom-call(f32[128,128]{1,0:T(8,128)S(1)} %convolution_subtract_fusion.9), custom_call_target="Cholesky" | custom-call | tf_op jit(solution)/shard_map/jit(cholesky)/cholesky | solution.py:12
  111.2 20.1 %custom-call.27 = f32[2,128,128]{1,2,0:T(8,128)S(1)} custom-call(f32[2,128,128]{2,1,0:T(8,128)S(1)} %get-tuple-element.71), custom_call_target="InvertDiagBlocksLowerTriangular" | custom-call | tf_op jit(solution)/shard_map/triangular_solve/custom-call.0 | solution.py:13
  133.4 11.7 %cholesky.290 = f32[128,128]{1,0:T(8,128)S(1)} custom-call(f32[128,128]{1,0:T(8,128)S(1)} %cholesky.425), custom_call_target="Cholesky" | custom-call | tf_op jit(solution)/shard_map/jit(cholesky)/cholesky | solution.py:12
  145.1 9.8 %custom-call.29 = f32[1,128,128]{1,2,0:T(8,128)S(1)} custom-call(f32[1,128,128]{2,1,0:T(8,128)S(1)} %get-tuple-element.146), custom_call_target="InvertDiagBlocksLowerTriangular" | custom-call | tf_op jit(solution)/shard_map/jit(cholesky)/cholesky | solution.py:12
  155.4 11.7 %cholesky.307 = f32[128,128]{1,0:T(8,128)S(1)} custom-call(f32[128,128]{1,0:T(8,128)S(1)} %convolution_subtract_fusion.7), custom_call_target="Cholesky" | custom-call | tf_op jit(solution)/shard_map/jit(cholesky)/cholesky | solution.py:12
  178.9 19.7 %custom-call.30 = f32[2,128,128]{1,2,0:T(8,128)S(1)} custom-call(f32[2,128,128]{2,1,0:T(8,128)S(1)} %get-tuple-element.73), custom_call_target="InvertDiagBlocksLowerTriangular" | custom-call | tf_op jit(solution)/shard_map/triangular_solve/custom-call.0 | solution.py:13
  198.6 37.3 %reduce-scatter.10.cloned.1.call-done = f32[32,256]{1,0:T(8,128)} async-done(((f32[256,256]{1,0:T(8,128)}), f32[32,256]{1,0:T(8,128)}) %reduce-scatter.10.cloned.1.call-update) | async-done | bytes 32784
  238.7 30.9 %all_gather.17 = f32[256,256]{1,0:T(8,128)S(1)} all-gather(f32[32,256]{1,0:T(8,128)S(1)} %maximum_multiply_fusion.1), channel_id=1, replica_groups=mesh['row'=8,'col'=4] {'row'}, dimensions={0}, use_global_device_ids=true | all-gather | bytes 294912 | tf_op jit(solution)/shard_map/all_gather | solution.py:55
  281.1 38.9 %psum.60 = f32[32,256]{0,1:T(8,128)S(1)} all-reduce(f32[32,256]{0,1:T(8,128)S(1)} %bitcast.279), channel_id=1, replica_groups=mesh['row'=8,'col'=4] {'row','col'}, use_global_device_ids=true, to_apply=%region_12.16 | all-reduce | flops 8192 | bytes 65536 | tf_op jit(solution)/shard_map/psum | solution.py:44
  321.2 11.7 %cholesky.324 = f32[128,128]{1,0:T(8,128)S(1)} custom-call(f32[128,128]{1,0:T(8,128)S(1)} %cholesky.428), custom_call_target="Cholesky" | custom-call | tf_op jit(solution)/shard_map/jit(cholesky)/cholesky | solution.py:12
  333.0 9.8 %custom-call.32 = f32[1,128,128]{1,2,0:T(8,128)S(1)} custom-call(f32[1,128,128]{2,1,0:T(8,128)S(1)} %get-tuple-element.142), custom_call_target="InvertDiagBlocksLowerTriangular" | custom-call | tf_op jit(solution)/shard_map/jit(cholesky)/cholesky | solution.py:12
  343.3 11.7 %cholesky.341 = f32[128,128]{1,0:T(8,128)S(1)} custom-call(f32[128,128]{1,0:T(8,128)S(1)} %convolution_subtract_fusion.5), custom_call_target="Cholesky" | custom-call | tf_op jit(solution)/shard_map/jit(cholesky)/cholesky | solution.py:12
  361.7 20.1 %custom-call.33 = f32[2,128,128]{1,2,0:T(8,128)S(1)} custom-call(f32[2,128,128]{2,1,0:T(8,128)S(1)} %get-tuple-element.75), custom_call_target="InvertDiagBlocksLowerTriangular" | custom-call | tf_op jit(solution)/shard_map/triangular_solve/custom-call.0 | solution.py:13
  383.8 11.7 %cholesky.358 = f32[128,128]{1,0:T(8,128)S(1)} custom-call(f32[128,128]{1,0:T(8,128)S(1)} %cholesky.431), custom_call_target="Cholesky" | custom-call | tf_op jit(solution)/shard_map/jit(cholesky)/cholesky | solution.py:12
  395.6 9.8 %custom-call.35 = f32[1,128,128]{1,2,0:T(8,128)S(1)} custom-call(f32[1,128,128]{2,1,0:T(8,128)S(1)} %get-tuple-element.138), custom_call_target="InvertDiagBlocksLowerTriangular" | custom-call | tf_op jit(solution)/shard_map/jit(cholesky)/cholesky | solution.py:12
  405.9 11.7 %cholesky.375 = f32[128,128]{1,0:T(8,128)S(1)} custom-call(f32[128,128]{1,0:T(8,128)S(1)} %convolution_subtract_fusion.3), custom_call_target="Cholesky" | custom-call | tf_op jit(solution)/shard_map/jit(cholesky)/cholesky | solution.py:12
  429.2 19.7 %custom-call.36 = f32[2,128,128]{1,2,0:T(8,128)S(1)} custom-call(f32[2,128,128]{2,1,0:T(8,128)S(1)} %get-tuple-element.77), custom_call_target="InvertDiagBlocksLowerTriangular" | custom-call | tf_op jit(solution)/shard_map/triangular_solve/custom-call.0 | solution.py:13
  449.0 38.3 %reduce-scatter.12.cloned.1.call-done = f32[32,256]{1,0:T(8,128)} async-done(((f32[256,256]{1,0:T(8,128)}), f32[32,256]{1,0:T(8,128)}) %reduce-scatter.12.cloned.1.call-update) | async-done | bytes 32784
  490.2 30.9 %all_gather.18 = f32[256,256]{1,0:T(8,128)S(1)} all-gather(f32[32,256]{1,0:T(8,128)S(1)} %maximum_multiply_fusion.3), channel_id=1, replica_groups=mesh['row'=8,'col'=4] {'row'}, dimensions={0}, use_global_device_ids=true | all-gather | bytes 294912 | tf_op jit(solution)/shard_map/all_gather | solution.py:55
  521.1 5.7 psum.61
  528.2 9.8 %fusion.4 = f32[256,32,128]{2,0,1:T(8,128)} fusion(f32[32,128,256]{2,1,0:T(8,128)} %param.8, f32[256,256]{1,0:T(8,128)S(1)} %broadcast_divide_fusion), kind=kOutput, calls=%fused_computation.40 | convolution fusion | flops 3221225472 | bytes 8650752 | tf_op jit(solution)/shard_map/kij,jr->kir/dot_general | solution.py:57
  538.1 8.2 %fusion = f32[256,1,128]{2,1,0:T(1,128)S(1)} fusion(f32[32,256,1]{0,2,1:T(1,128)S(1)} %copy.65, f32[256,32,128]{2,0,1:T(8,128)} %fusion.4), kind=kOutput, calls=%fused_computation.14 | convolution fusion | flops 12582912 | bytes 4358144 | tf_op jit(solution)/shard_map/kir,kr->ir/dot_general | solution.py:58
  547.1 22.3 %all-reduce.9.cloned.1.call-done = f32[256,256]{0,1:T(8,128)} async-done(((f32[256,256]{0,1:T(8,128)}), f32[256,256]{0,1:T(8,128)}) %all-reduce.9.cloned.1.call-update) | async-done | bytes 262160 | tf_op jit(solution)/shard_map/psum | solution.py:29
  570.6 11.7 %cholesky.392 = f32[128,128]{1,0:T(8,128)S(1)} custom-call(f32[128,128]{1,0:T(8,128)S(1)} %cholesky.434), custom_call_target="Cholesky" | custom-call | tf_op jit(solution)/shard_map/jit(cholesky)/cholesky | solution.py:12
  582.3 9.8 %custom-call.38 = f32[1,128,128]{1,2,0:T(8,128)S(1)} custom-call(f32[1,128,128]{2,1,0:T(8,128)S(1)} %get-tuple-element.134), custom_call_target="InvertDiagBlocksLowerTriangular" | custom-call | tf_op jit(solution)/shard_map/jit(cholesky)/cholesky | solution.py:12
  592.6 11.7 %cholesky.409 = f32[128,128]{1,0:T(8,128)S(1)} custom-call(f32[128,128]{1,0:T(8,128)S(1)} %convolution_subtract_fusion.1), custom_call_target="Cholesky" | custom-call | tf_op jit(solution)/shard_map/jit(cholesky)/cholesky | solution.py:12
  611.1 19.9 %custom-call.39 = f32[2,128,128]{1,2,0:T(8,128)S(1)} custom-call(f32[2,128,128]{2,1,0:T(8,128)S(1)} %get-tuple-element.79), custom_call_target="InvertDiagBlocksLowerTriangular" | custom-call | tf_op jit(solution)/shard_map/triangular_solve/custom-call.0 | solution.py:13
  639.3 21.4 %psum.63 = f32[256]{0:T(256)S(1)} all-reduce(f32[256]{0:T(256)S(1)} %multiply_reduce_fusion.6), channel_id=1, replica_groups=mesh['row'=8,'col'=4] {'row'}, use_global_device_ids=true, to_apply=%region_20.24 | all-reduce | flops 256 | bytes 2048 | tf_op jit(solution)/shard_map/psum | solution.py:63
  (196 shorter events, 100.9 us)
Async XLA Ops:
  8.0 0.9 copy-start
  8.0 60.2 %all-gather.3.cloned.1.call-start = ((), (), s32[]{:S(2)}) async-start(), calls=%async_computation.6 | async-start | bytes 2359296 | tf_op jit(solution)/shard_map/all_gather | solution.py:38
  10.1 60.1 %all-reduce.5.cloned.1.call-start = ((), (), s32[]{:S(2)}) async-start(), calls=%async_computation.3 | async-start | bytes 524288 | tf_op jit(solution)/shard_map/psum | solution.py:40
  12.5 223.4 %reduce-scatter.10.cloned.1.call-start = ((), (), s32[]{:S(2)}) async-start(), calls=%async_computation.7 | async-start | bytes 294912
  173.3 146.7 %all-reduce.7.cloned.1.call-start = ((), (), s32[]{:S(2)}) async-start(), calls=%async_computation.4 | async-start | bytes 524288 | tf_op jit(solution)/shard_map/psum | solution.py:29
  276.7 210.6 %reduce-scatter.12.cloned.1.call-start = ((), (), s32[]{:S(2)}) async-start(), calls=%async_computation.8 | async-start | bytes 294912
  383.2 65.7 %copy-start.2 = (f32[32,256]{1,0:T(8,128)}, f32[32,256]{1,0:T(8,128)S(1)}, u32[]{:S(2)}) copy-start(f32[32,256]{1,0:T(8,128)S(1)} %fusion.78) | copy-start | bytes 98308
  423.8 145.6 %all-reduce.9.cloned.1.call-start = ((), (), s32[]{:S(2)}) async-start(), calls=%async_computation.5 | async-start | bytes 524288 | tf_op jit(solution)/shard_map/psum | solution.py:29
  526.9 11.2 %copy-start.1 = (f32[256,256]{1,0:T(8,128)}, f32[256,256]{1,0:T(8,128)S(1)}, u32[]{:S(2)}) copy-start(f32[256,256]{1,0:T(8,128)S(1)} %broadcast_divide_fusion) | copy-start | bytes 786436
  538.0 93.0 %reduce-scatter.14.cloned.1.call-start = ((), (), s32[]{:S(2)}) async-start(), calls=%async_computation.9 | async-start | bytes 163840
  660.7 0.7 copy-start.3
Sparse Core Ops, SparseCore 0:
  10.9 51.8 all-gather.2
  173.5 62.3 reduce-scatter.9
  423.9 63.4 reduce-scatter.11
Sparse Core Ops, SparseCore 1:
  13.4 34.8 all-reduce.4
  276.8 31.2 all-reduce.6
  538.1 31.2 all-reduce.8
  572.4 19.8 reduce-scatter.13
